TPU v7x, 768 devices: a whole 4x8x12 slice. The times are simulated.
768 devices in a mesh: dp: 192 (over z, y, core), tensor: 4 (over x).
Axes of the slice: x: 4, y: 8, z: 12, core: 2. Of those that a mesh axis runs over, the one named last changes fastest.
Arguments:
- activations: bfloat16 [49152, 27648], P('dp', 'tensor'), may hold values from -24 to 24
- output_gradient: bfloat16 [49152, 5120], P('dp', 'tensor'), may hold values from -6 to 6
- adapter_a: bfloat16 [4, 6912, 128], P('tensor', 'dp'), may hold values from -0.0390625 to 0.0390625
- adapter_b: bfloat16 [128, 5120], P(None, 'tensor'), may hold values from -0.078125 to 0.078125
- log_ratio: float32 [49152], P('dp'), may hold values from -1.5 to 1.5
- lengths: int32 [3, 16], replicated, may hold values from 1 to 1024, as said below
- rewards: int32 [3, 16], replicated, may hold values from 0 to 10
Outputs:
- grad_a: float32 [4, 6912, 128], P('tensor', 'dp')
- adapter_b_gradient: float32 [128, 5120], P(None, 'tensor')
- loss: float32 [], replicated
Inputs may be any that keep to these rules, and one draw needn't show every extreme that they name: `lengths`: in every group some rollout has length 1024.
All inputs are finite; a program needn't handle non-finite values.
Results may differ from a plain program's by a relative error of at most 0.0067.
Values may be sent and summed in bfloat16 or wider, within the bound.
A program may use at most 64 MiB of HBM per device.

v0:
```python
import jax
import jax.numpy as jnp
from jax import lax
from jax.sharding import Mesh
from jax.sharding import PartitionSpec as P

DP = ("dp_0", "dp_1", "dp_2")


clip_eps = 0.2
adapter_scale_factor = 2.0


def laid_out(blocks, dim):
    blocks = jnp.moveaxis(blocks, 0, dim)
    lengths = blocks.shape
    return blocks.reshape(*lengths[:dim], lengths[dim] * lengths[dim + 1], *lengths[dim + 2 :])


def stacked_from(array, axes, turns):
    blocks = array
    for k in turns:
        blocks = lax.all_gather(blocks, axes[k])
    done = turns[::-1]
    back = [done.index(k) for k in range(len(axes))]
    blocks = blocks.transpose(*back, *range(len(axes), blocks.ndim))
    return blocks.reshape(-1, *array.shape)


def gathered_by_axis(array, axes, turns, dim):
    return laid_out(stacked_from(array, axes, turns), dim)


def split_up(array, dim, devices):
    before, after = (array.shape[:dim], array.shape[dim + 1 :])
    return jnp.moveaxis(array.reshape(*before, devices, -1, *after), dim, 0)


def sent_and_summed(array, axis, dim):
    blocks = split_up(array, dim, lax.axis_size(axis))
    arrived = lax.all_to_all(blocks, axis, split_axis=0, concat_axis=0, tiled=True)
    return arrived.sum(axis=0)


def in_one_piece(arrays, axis, dim, along):
    ends, at = ([], 0)
    for a in arrays[:-1]:
        at += a.shape[along]
        ends.append(at)
    both = jnp.concatenate(arrays, axis=along)
    return tuple(jnp.split(sent_and_summed(both, axis, dim), ends, axis=along))


def packed_total(arrays, axis):
    ends = [0]
    for a in arrays:
        ends.append(ends[-1] + a.size)
    running = lax.psum(jnp.concatenate([a.ravel() for a in arrays]), axis)
    return tuple((running[b:e].reshape(a.shape) for a, b, e in zip(arrays, ends, ends[1:])))


def token_terms(length_row, reward_row, log_ratio, offset):
    reward = reward_row.astype(jnp.float32)
    center = jnp.mean(reward)
    spread = jnp.mean((reward - center) * (reward - center))
    advantage = (reward - center) / jnp.sqrt(spread + 1.0)
    ends = jnp.cumsum(length_row)
    starts = ends - length_row
    slots = jnp.arange(log_ratio.shape[0], dtype=jnp.int32) + offset
    member = ((slots[None, :] >= starts[:, None]) & (slots[None, :] < ends[:, None])).astype(
        jnp.float32
    )
    live = jnp.sum(member, axis=0)
    token_adv = jnp.sum(member * advantage[:, None], axis=0)
    ratio = jnp.exp(log_ratio)
    unclipped = ratio * token_adv
    clipped = jnp.clip(ratio, 1.0 - clip_eps, 1.0 + clip_eps) * token_adv
    token_loss = -jnp.minimum(unclipped, clipped)
    slope = jnp.where(unclipped <= clipped, -unclipped, jnp.zeros_like(unclipped))
    return (live * slope, jnp.sum(live * token_loss), jnp.sum(live))


def local(activations, output_gradient, adapter_a, adapter_b, log_ratio, lengths, rewards):
    tokens = activations.shape[0]
    groups = lengths.shape[0]
    per_group = lax.axis_size(DP) // groups
    position = lax.axis_index(DP)
    group_id = position // per_group
    offset = position % per_group * tokens
    length_row = lax.dynamic_index_in_dim(lengths, group_id, 0, keepdims=False)
    reward_row = lax.dynamic_index_in_dim(rewards, group_id, 0, keepdims=False)
    token_coefficient, loss_local, live_count = token_terms(
        length_row, reward_row, log_ratio, offset
    )
    columns = activations
    partial_low = jnp.dot(
        columns,
        gathered_by_axis(adapter_a, DP, (0, 1, 2), 1)[0],
        preferred_element_type=jnp.float32,
    )
    partial_back = lax.dot_general(
        output_gradient, adapter_b, (((1,), (1,)), ((), ())), preferred_element_type=jnp.float32
    )
    share_low, share_back = in_one_piece((partial_low, partial_back), "tensor", 0, 1)
    share_rows = share_low.shape[0]
    share_start = lax.axis_index("tensor") * share_rows
    share_coeff = lax.dynamic_slice_in_dim(token_coefficient, share_start, share_rows, 0)
    share_error = (
        (adapter_scale_factor * share_coeff[:, None] * share_back)
        .astype(jnp.bfloat16)
        .astype(jnp.float32)
    )
    share_weighted = share_coeff[:, None] * share_low
    error_whole, weighted_error = (
        lax.all_gather(share_error, "tensor", axis=0, tiled=True),
        lax.all_gather(share_weighted, "tensor", axis=0, tiled=True),
    )
    error_rows = error_whole.astype(jnp.bfloat16)
    local_adapter_b_gradient = adapter_scale_factor * jnp.einsum(
        "tr,td->rd",
        weighted_error,
        output_gradient.astype(jnp.float32),
        precision=lax.Precision.HIGHEST,
    )
    columns = activations
    grad_a = lax.psum_scatter(
        lax.dot_general(
            columns, error_rows, (((0,), (0,)), ((), ())), preferred_element_type=jnp.float32
        ),
        DP,
        scatter_dimension=0,
        tiled=True,
    )
    grad_b_sum, loss_sum, live_sum = packed_total(
        (local_adapter_b_gradient, loss_local, live_count), DP
    )
    factor = groups / live_sum
    return ((factor * grad_a)[None], factor * grad_b_sum, factor * loss_sum)


def solution(mesh):
    split = Mesh(
        mesh.devices.reshape(12, 8, 2, mesh.shape["tensor"]), ("dp_0", "dp_1", "dp_2", "tensor")
    )
    in_specs = (
        P(DP, "tensor"),
        P(DP, "tensor"),
        P("tensor", DP, None),
        P(None, "tensor"),
        P(DP),
        P(),
        P(),
    )
    out_specs = (P("tensor", DP, None), P(None, "tensor"), P())
    return jax.shard_map(local, mesh=split, in_specs=in_specs, out_specs=out_specs, check_vma=False)
```

profile of v0, /device:TPU:1, one launch (start us, length us, event | category | flops | bytes accessed | tf_op | source)
XLA Modules:
  0.0 487.8 jit_solution(7911351813089679552)
XLA Ops:
  7.2 28.6 %all-gather = bf16[12,36,128]{2,1,0:T(8,128)(2,1)S(1)} all-gather(bf16[1,36,128]{2,1,0:T(8,128)(2,1)} %param.9), channel_id=2, replica_groups=mesh['dp_0'=12,'dp_1'=8,'dp_2'=2,'tensor'=4] {'dp_0'}, dimensions={0}, use_global_device_ids=true | all-gather | bytes 119808 | tf_op jit(solution)/shard_map/all_gather | solution.py:23
  35.9 22.8 %all-gather.1 = bf16[96,36,128]{2,1,0:T(8,128)(2,1)S(1)} all-gather(bf16[12,36,128]{2,1,0:T(8,128)(2,1)S(1)} %all-gather), channel_id=3, replica_groups=mesh['dp_0'=12,'dp_1'=8,'dp_2'=2,'tensor'=4] {'dp_1'}, dimensions={0}, use_global_device_ids=true | all-gather | bytes 995328 | tf_op jit(solution)/shard_map/all_gather | solution.py:23
  58.7 1.3 copy.30
  62.6 0.7 fusion.5
  63.5 0.7 divide_bitcast_fusion
  64.2 0.7 bitcast_subtract_fusion
  64.9 0.7 convert_reduce_fusion
  65.6 2.2 fusion.8
  67.8 18.8 %all-gather.5.cloned.1.call-done = bf16[16,12,1,36,128]{4,0,3,2,1:T(8,128)(2,1)} async-done(((bf16[8,12,1,36,128]{4,0,3,2,1:T(8,128)(2,1)}), bf16[16,12,1,36,128]{4,0,3,2,1:T(8,128)(2,1)}) %all-gather.5.cloned.1.call-update) | async-done | bytes 1769488 | tf_op jit(solution)/shard_map/all_gather | solution.py:23
  86.6 3.2 copy.31
  89.8 3.7 squeeze_reshape_transpose_reshape.3
  93.6 2.8 fusion.7
  96.4 0.7 pad_maximum_fusion
  97.1 1.8 copy.32
  98.9 4.0 all-to-all-start
  103.6 0.7 broadcast_multiply_fusion
  104.3 4.9 %all-to-all-done = f32[4,64,256]{2,1,0:T(8,128)} async-done(((f32[4,64,256]{2,1,0:T(8,128)}), f32[4,64,256]{2,1,0:T(8,128)}, u32[]{:S(2)}, u32[]{:S(2)}) %all-to-all-start) | async-done | bytes 262176 | tf_op jit(solution)/shard_map/all_to_all | solution.py:41
  109.3 1.6 reduce_sum.67
  110.9 0.9 slice_multiply_fusion.2
  111.7 9.5 %all_gather.30 = f32[256,128]{1,0:T(8,128)S(1)} all-gather(f32[64,128]{1,0:T(8,128)S(1)} %get-tuple-element.30), channel_id=1, replica_groups=mesh['dp_0'=12,'dp_1'=8,'dp_2'=2,'tensor'=4] {'tensor'}, dimensions={0}, use_global_device_ids=true | all-gather | bytes 163840 | tf_op jit(solution)/shard_map/all_gather | solution.py:116
  121.2 2.4 convolution_multiply_fusion
  123.6 2.0 reshape.78
  125.6 9.2 %all_gather.31 = bf16[256,128]{1,0:T(8,128)(2,1)S(1)} all-gather(bf16[64,128]{1,0:T(8,128)(2,1)S(1)} %get-tuple-element.31), channel_id=1, replica_groups=mesh['dp_0'=12,'dp_1'=8,'dp_2'=2,'tensor'=4] {'tensor'}, dimensions={0}, use_global_device_ids=true | all-gather | bytes 81920 | tf_op jit(solution)/shard_map/all_gather | solution.py:115
  134.8 2.5 convolution_bitcast_fusion
  137.3 8.5 %concatenate.7 = f32[163842]{0:T(1024)} concatenate(f32[163840]{0:T(1024)} %reshape.78, f32[1]{0:T(128)} %bitcast.7, f32[1]{0:T(128)} %bitcast.8), dimensions={0} | concatenate | bytes 1310736 | tf_op jit(solution)/shard_map/concatenate | solution.py:58
  145.7 1.3 dynamic-slice
  147.7 322.3 %all-reduce.4.cloned.1.call-done = (f32[6912,128]{0,1:T(8,128)}, f32[163842]{0:T(1024)}) async-done(((f32[6912,128]{0,1:T(8,128)}, f32[163842]{0:T(1024)}), (f32[6912,128]{0,1:T(8,128)}, f32[163842]{0:T(1024)})) %all-reduce.4.cloned.1.call-update) | async-done | bytes 4194328
  470.0 1.3 fusion.6
  472.0 2.0 slice_multiply_fusion
  474.6 2.0 mul.106
  476.7 1.6 fusion
  478.3 1.5 copy.33
  (19 shorter events, 2.2 us)
Async XLA Ops:
  7.2 86.4 %copy-start = (bf16[256,6912]{1,0:T(8,128)(2,1)S(1)}, bf16[256,6912]{1,0:T(8,128)(2,1)}, u32[]{:S(2)}) copy-start(bf16[256,6912]{1,0:T(8,128)(2,1)} %param.7) | copy-start | bytes 10616836
  7.2 52.8 %copy-start.3 = (s32[3,16]{1,0:T(4,128)S(1)}, s32[3,16]{1,0:T(4,128)}, u32[]{:S(2)}) copy-start(s32[3,16]{1,0:T(4,128)} %param.13) | copy-start | bytes 580
  7.2 79.4 %all-gather.5.cloned.1.call-start = ((), (), s32[]{:S(2)}) async-start(), calls=%async_computation.1 | async-start | bytes 2654208 | tf_op jit(solution)/shard_map/all_gather | solution.py:23
  93.6 2.8 copy-start.1
  93.6 9.4 %copy-start.2 = (f32[256]{0:T(256)S(1)}, f32[256]{0:T(256)}, u32[]{:S(2)}) copy-start(f32[256]{0:T(256)} %param.11) | copy-start | bytes 3076
  98.9 10.3 %all-to-all-start = ((f32[4,64,256]{2,1,0:T(8,128)}), f32[4,64,256]{2,1,0:T(8,128)}, u32[]{:S(2)}, u32[]{:S(2)}) async-start(f32[4,64,256]{2,1,0:T(8,128)} %bitcast.34), calls=%async_computation | async-start | bytes 524288 | tf_op jit(solution)/shard_map/all_to_all | solution.py:41
  103.0 367.0 %all-reduce.4.cloned.1.call-start = ((), (), s32[]{:S(2)}) async-start(), calls=%async_computation.2 | async-start | bytes 8396800
Sparse Core Ops, SparseCore 0:
  60.1 26.4 all-gather.4
  145.9 324.0 all-reduce.3
where the time goes:
time: 489 us; the launch traced here: 488 us
  waiting for transfers between devices  346 us (71%)
  blocking collectives  70.1 us (14%)
  local copies, waits for them, and re-layouts  27.4 us (6%)
  between operations  18.6 us (4%)
  other arithmetic  11.5 us (2%)
  matrix products  9.92 us (2%)
    unnamed x3, waiting for transfers between devices  322 us
    all_gather x2, blocking collectives, stacked_from(): blocks = lax.all_gather(blocks, axes[k])  51.4 us
    all_gather x1, waiting for transfers between devices, stacked_from(): blocks = lax.all_gather(blocks, axes[k])  18.8 us
  transfers between devices with their start and end apart: 3, of which 3 were waited for; matrix products, arithmetic and copies ran while one was open for 2% of the time, Pallas kernels for 0%

commit v1 on v0

v1 whole, which is shorter than its diff:
```python
import functools

import jax
import jax.numpy as jnp
from jax import lax
from jax.experimental import pallas as pl
from jax.experimental.pallas import tpu as pltpu
from jax.sharding import Mesh
from jax.sharding import PartitionSpec as P

Z, Y, C, X = "dp_0", "dp_1", "dp_2", "tensor"
DP = (Z, Y, C)
BY_AXIS = pl.DeviceIdType.MESH

clip_eps = 0.2
adapter_scale_factor = 2.0
UNIT = 8
LANES = 128


def units_split(total, ny, nz):
    pairs = [
        (a, (total - ny * a) // nz)
        for a in range(1, total // ny + 1)
        if total > ny * a and (total - ny * a) % nz == 0
    ]
    return min(pairs, key=lambda p: abs(ny * p[0] - 0.55 * total))


def far_first(n):
    return sorted(range(1, n), key=lambda k: -min(k, n - k))


def kernel(
    dims,
    act_hbm, og_hbm, b_hbm, a_ref, lr_ref, len_ref, rew_ref,
    ga_ref, gb_ref, loss_ref,
    act, og, bv, coeff_v, back_v, low_v, xb, xl,
    abuf, apart, afull, err_v, pfull, psend, precv, rrecv, rsend, rown, rownb, rmin,
    gbs, usend, urecv, uown, umin, umaj, ufin, ufinp, lmin, lmaj, lcore,
    load_s, xs, xr, as_, ar, aring_s, aring_r, apart_s, apart_r,
    ps, pr, rring_s, rring_r, rmin_s, rmin_r,
    up_s, up_r, um_s, um_r, uj_s, uj_r, uf_s, uf_r, ufp_s, ufp_r,
    lm_s, lm_r, lj_s, lj_r, lc_s, lc_r,
):
    nz, ny, nx, groups, rollouts, rows, blocks, upcs = dims
    z, y, core, x = (lax.axis_index(n) for n in (Z, Y, C, X))
    tokens = act.shape[0]
    zy_all = nz * ny
    per_block = zy_all // blocks
    kb = per_block * 2 * rows
    size = {Z: nz, Y: ny, X: nx}

    def to(axis, index):
        return {axis: index}

    def remote(src, dst, ssem, rsem, axis, index):
        return pltpu.make_async_remote_copy(
            src_ref=src, dst_ref=dst, send_sem=ssem, recv_sem=rsem,
            device_id=to(axis, index), device_id_type=BY_AXIS,
        )

    sent = []

    def start(copy):
        copy.start()
        sent.append(copy)

    barrier = pltpu.get_barrier_semaphore()
    greet = 1
    pl.semaphore_signal(barrier, inc=1, device_id=to(C, 1 - core), device_id_type=BY_AXIS)
    for axis, me in ((Z, z), (Y, y), (X, x)):
        for k in far_first(size[axis]):
            pl.semaphore_signal(
                barrier, inc=1, device_id=to(axis, lax.rem(me + k, size[axis])), device_id_type=BY_AXIS
            )
            greet += 1
    load_og = pltpu.make_async_copy(og_hbm, og, load_s.at[0])
    load_b = pltpu.make_async_copy(b_hbm, bv, load_s.at[1])
    load_act = pltpu.make_async_copy(act_hbm, act, load_s.at[2])
    load_b.start()
    load_og.start()
    load_act.start()

    trows = tokens // LANES
    dpi = (z * ny + y) * 2 + core
    per_group = zy_all * 2 // groups
    g = dpi // per_group
    offset = (dpi % per_group) * tokens
    shape = (trows, LANES)
    slots = (
        lax.broadcasted_iota(jnp.int32, shape, 0) * LANES
        + lax.broadcasted_iota(jnp.int32, shape, 1)
        + offset
    )
    rewards = [jnp.full(shape, rew_ref[g, i], jnp.int32).astype(jnp.float32) for i in range(rollouts)]
    center = sum(rewards[1:], rewards[0]) / rollouts
    spread = sum([(r - center) * (r - center) for r in rewards]) / rollouts
    scale = jnp.sqrt(spread + 1.0)
    live = jnp.zeros(shape, jnp.float32)
    token_adv = jnp.zeros(shape, jnp.float32)
    begin = jnp.zeros(shape, jnp.int32)
    for i in range(rollouts):
        end = begin + jnp.full(shape, len_ref[g, i], jnp.int32)
        member = ((slots >= begin) & (slots < end)).astype(jnp.float32)
        live = live + member
        token_adv = token_adv + member * ((rewards[i] - center) / scale)
        begin = end
    ratio = jnp.exp(lr_ref[...])
    unclipped = ratio * token_adv
    clipped = jnp.clip(ratio, 1.0 - clip_eps, 1.0 + clip_eps) * token_adv
    token_loss = -jnp.minimum(unclipped, clipped)
    slope = jnp.where(unclipped <= clipped, -unclipped, jnp.zeros_like(unclipped))
    coeff = live * slope
    loss_row = jnp.sum(live * token_loss, axis=0, keepdims=True)
    for t in range(trows):
        row = jnp.broadcast_to(coeff[t : t + 1, :], (LANES, LANES))
        coeff_v[t * LANES : (t + 1) * LANES, :] = row.T
    total_len = jnp.zeros((UNIT, LANES), jnp.int32)
    for gi in range(groups):
        for i in range(rollouts):
            total_len = total_len + jnp.full((UNIT, LANES), len_ref[gi, i], jnp.int32)
    factor = groups / total_len.astype(jnp.float32)

    load_b.wait()
    load_og.wait()
    partial_back = lax.dot_general(
        og[...], bv[...], (((1,), (1,)), ((), ())), preferred_element_type=jnp.float32
    )
    xb[x] = partial_back.astype(jnp.bfloat16)
    pl.semaphore_wait(barrier, greet)

    def x_send(buf, base):
        for k in far_first(nx):
            start(remote(buf.at[x], buf.at[x], xs.at[base + k], xr.at[base + k], X, lax.rem(x + k, nx)))

    def x_sum(buf, base):
        for k in range(1, nx):
            src = lax.rem(x - k + nx, nx)
            remote(buf.at[x], buf.at[src], xs.at[base + k], xr.at[base + k], X, src).wait_recv()
        return sum([buf[i].astype(jnp.float32) for i in range(nx)])

    def body(c, maj, min_):
        nmaj, nmin = size[maj], size[min_]
        mj = z if maj == Z else y
        mn = y if maj == Z else z
        hp = nmaj // 2
        hm = nmaj - 1 - hp
        upc = upcs[c]
        oc = 1 - c
        o_nmin = nmaj

        def wrap(i):
            return lax.rem(i + 2 * nmaj, nmaj)

        def zy(d, m):
            return d * ny + m if c == 0 else m * ny + d

        def min_send(src_of, buf, ssem, rsem):
            for k in far_first(nmin):
                t = lax.rem(mn + k, nmin)
                start(remote(src_of(t), buf(mn), ssem.at[k], rsem.at[k], min_, t))

        def min_wait(src_of, buf, ssem, rsem, each=None):
            for k in far_first(nmin)[::-1]:
                f = lax.rem(mn - k + nmin, nmin)
                remote(src_of(f), buf(f), ssem.at[k], rsem.at[k], min_, f).wait_recv()
                if each is not None:
                    each(f)

        def maj_send(src, buf, ssem, rsem):
            for k in far_first(nmaj):
                t = lax.rem(mj + k, nmaj)
                start(remote(src, buf(mj), ssem.at[k], rsem.at[k], maj, t))

        def maj_wait(src, buf, ssem, rsem):
            for k in far_first(nmaj)[::-1]:
                f = lax.rem(mj - k + nmaj, nmaj)
                remote(src, buf(f), ssem.at[k], rsem.at[k], maj, f).wait_recv()

        def a_chunk(d):
            return abuf.at[pl.ds(d * nmin, nmin)]

        def a_first():
            own = mj * nmin + mn
            abuf[own] = a_ref[...]
            min_send(lambda t: a_ref, lambda i: abuf.at[mj * nmin + i], as_, ar)

        def a_first_wait():
            min_wait(lambda t: a_ref, lambda i: abuf.at[mj * nmin + i], as_, ar)

        def a_share(d, slot):
            start(remote(a_chunk(d), apart.at[pl.ds(d * nmin, nmin)], apart_s.at[slot], apart_r.at[slot], C, oc))

        def a_unpack(d):
            for m in range(nmin):
                afull[zy(d, m), c * rows : (c + 1) * rows, :] = abuf[d * nmin + m].astype(jnp.float32)

        def a_ring_send(s):
            if s < hp:
                d = wrap(mj - s)
                start(remote(a_chunk(d), a_chunk(d), aring_s.at[s], aring_r.at[s], maj, wrap(mj + 1)))
            if s < hm:
                d = wrap(mj + s)
                start(remote(a_chunk(d), a_chunk(d), aring_s.at[hp + s], aring_r.at[hp + s], maj, wrap(mj - 1)))

        def a_ring_wait(s):
            if s < hp:
                d = wrap(mj - 1 - s)
                remote(a_chunk(d), a_chunk(d), aring_s.at[s], aring_r.at[s], maj, wrap(mj + 1)).wait_recv()
            if s < hm:
                d = wrap(mj + 1 + s)
                remote(a_chunk(d), a_chunk(d), aring_s.at[hp + s], aring_r.at[hp + s], maj, wrap(mj - 1)).wait_recv()

        def a_ring_use(s):
            if s < hp:
                a_share(wrap(mj - 1 - s), 1 + s)
                a_unpack(wrap(mj - 1 - s))
            if s < hm:
                a_share(wrap(mj + 1 + s), 1 + hp + s)
                a_unpack(wrap(mj + 1 + s))

        def a_partner():
            n2, m2 = nmin, nmaj
            hp2 = n2 // 2
            order = [(0, 0)]
            for s in range(hp2):
                order.append((1 + s, -1 - s))
                if s < n2 - 1 - hp2:
                    order.append((1 + hp2 + s, 1 + s))
            for slot, step in order:
                d = lax.rem(mn + step + 2 * n2, n2)
                part = apart.at[pl.ds(d * m2, m2)]
                remote(part, part, apart_s.at[slot], apart_r.at[slot], C, oc).wait_recv()
                for m in range(m2):
                    at = d * ny + m if oc == 0 else m * ny + d
                    afull[at, oc * rows : (oc + 1) * rows, :] = apart[d * m2 + m].astype(jnp.float32)

        def p_block(j):
            got = lax.dot_general(
                act[:, j * kb : (j + 1) * kb], err_v[...], (((0,), (0,)), ((), ())),
                preferred_element_type=jnp.float32,
            )
            pfull[j * per_block : (j + 1) * per_block] = got.reshape(per_block, 2 * rows, LANES)
            for i in range(j * per_block, (j + 1) * per_block):
                zi, yi = divmod(i, ny)
                at = zi * ny + yi if oc == 0 else yi * nz + zi
                psend[at] = pfull[i, oc * rows : (oc + 1) * rows, :].astype(jnp.bfloat16)

        def p_copy():
            return remote(psend, precv, ps.at[0], pr.at[0], C, oc)

        def r_term(d, m):
            mine = pfull[zy(d, m), c * rows : (c + 1) * rows, :]
            return mine + precv[d * nmin + m].astype(jnp.float32)

        def r_copy(s, plus):
            slot = s if plus else hp + s
            return remote(
                rsend.at[pl.ds(slot * nmin, nmin)], rrecv.at[pl.ds(slot * nmin, nmin)],
                rring_s.at[slot], rring_r.at[slot], maj, wrap(mj + 1) if plus else wrap(mj - 1),
            )

        def r_ring(s):
            for plus, h in ((True, hp), (False, hm)):
                if s >= h:
                    continue
                slot = s if plus else hp + s
                d = wrap(mj + (hp - s)) if plus else wrap(mj - (hm - s))
                if s:
                    r_copy(s - 1, plus).wait_recv()
                for m in range(nmin):
                    v = r_term(d, m)
                    if s:
                        v = v + rrecv[(slot - 1) * nmin + m].astype(jnp.float32)
                    rsend[slot * nmin + m] = v.astype(jnp.bfloat16)
                start(r_copy(s, plus))

        def r_end():
            r_copy(hp - 1, True).wait_recv()
            if hm:
                r_copy(hm - 1, False).wait_recv()
            for m in range(nmin):
                v = r_term(mj, m) + rrecv[(hp - 1) * nmin + m].astype(jnp.float32)
                if hm:
                    v = v + rrecv[(hp + hm - 1) * nmin + m].astype(jnp.float32)
                rown[m] = v
                rownb[m] = v.astype(jnp.bfloat16)
            min_send(lambda t: rownb.at[t], lambda i: rmin.at[i], rmin_s, rmin_r)

        def r_out():
            rmin[mn] = jnp.zeros((rows, LANES), jnp.bfloat16)
            min_wait(lambda t: rownb.at[t], lambda i: rmin.at[i], rmin_s, rmin_r)
            total = rown[mn]
            for m in range(nmin):
                total = total + rmin[m].astype(jnp.float32)
            ga_ref[...] = total * factor[:1, :]

        wide = og.shape[1] // LANES
        first = 0 if c == 0 else ny * upcs[0]
        o_first = 0 if oc == 0 else ny * upcs[0]
        mine_n, other_n = nmin * upc, nmaj * upcs[oc]

        def unit_at(u):
            r, k = divmod(u, wide)
            return slice(r * UNIT, (r + 1) * UNIT), slice(k * LANES, (k + 1) * LANES)

        def u_copy():
            return remote(
                usend.at[pl.ds(0, other_n)], urecv.at[pl.ds(0, other_n)], up_s.at[0], up_r.at[0], C, oc
            )

        def u_from_partner():
            return remote(
                usend.at[pl.ds(0, mine_n)], urecv.at[pl.ds(0, mine_n)], up_s.at[0], up_r.at[0], C, oc
            )

        def u_local():
            low = x_sum(xl, nx)
            weighted = (coeff_v[...] * low).astype(jnp.bfloat16)
            gbs[...] = adapter_scale_factor * lax.dot_general(
                weighted, og[...], (((0,), (0,)), ((), ())), preferred_element_type=jnp.float32
            )
            for j in range(other_n):
                usend[j] = gbs[unit_at(o_first + j)].astype(jnp.bfloat16)
            start(u_copy())

        def u_chunk(ref, i):
            return ref.at[pl.ds(i * upc, upc)]

        def u_scatter():
            u_from_partner().wait_recv()
            for j in range(mine_n):
                v = gbs[unit_at(first + j)] + urecv[j].astype(jnp.float32)
                uown[j] = v.astype(jnp.bfloat16)
            min_send(lambda t: u_chunk(uown, t), lambda i: u_chunk(umin, i), um_s, um_r)

        def u_spread():
            for j in range(upc):
                umin[mn * upc + j] = uown[mn * upc + j]
            min_wait(lambda t: u_chunk(uown, t), lambda i: u_chunk(umin, i), um_s, um_r)
            for j in range(upc):
                v = sum([umin[m * upc + j].astype(jnp.float32) for m in range(nmin)])
                umaj[mj * upc + j] = v.astype(jnp.bfloat16)
            maj_send(u_chunk(umaj, mj), lambda i: u_chunk(umaj, i), uj_s, uj_r)

        def u_share(i, slot):
            start(remote(u_chunk(ufin, i), u_chunk(ufinp, i), ufp_s.at[slot], ufp_r.at[slot], C, oc))

        def u_gather():
            maj_wait(u_chunk(umaj, mj), lambda i: u_chunk(umaj, i), uj_s, uj_r)
            for j in range(upc):
                v = sum([umaj[m * upc + j].astype(jnp.float32) for m in range(nmaj)])
                ufin[mn * upc + j] = v.astype(jnp.bfloat16)
            min_send(lambda t: u_chunk(ufin, mn), lambda i: u_chunk(ufin, i), uf_s, uf_r)
            u_share(mn, 0)

        def u_out():
            for k in far_first(nmin)[::-1]:
                f = lax.rem(mn - k + nmin, nmin)
                remote(u_chunk(ufin, mn), u_chunk(ufin, f), uf_s.at[k], uf_r.at[k], min_, f).wait_recv()
                u_share(f, k)
            for j in range(mine_n):
                gb_ref[unit_at(first + j)] = ufin[j].astype(jnp.float32) * factor
            o_upc, n2 = upcs[oc], nmaj
            for k in [0] + far_first(n2)[::-1]:
                f = lax.rem(mj - k + n2, n2)
                part = ufinp.at[pl.ds(f * o_upc, o_upc)]
                remote(part, part, ufp_s.at[k], ufp_r.at[k], C, oc).wait_recv()
            for j in range(other_n):
                gb_ref[unit_at(o_first + j)] = ufinp[j].astype(jnp.float32) * factor

        def l_first():
            lmin[mn] = jnp.broadcast_to(loss_row, (UNIT, LANES))
            min_send(lambda t: lmin.at[mn], lambda i: lmin.at[i], lm_s, lm_r)

        def l_second():
            min_wait(lambda t: lmin.at[mn], lambda i: lmin.at[i], lm_s, lm_r)
            lmaj[mj] = sum([lmin[m] for m in range(nmin)])
            maj_send(lmaj.at[mj], lambda i: lmaj.at[i], lj_s, lj_r)

        def l_core():
            return remote(lcore.at[c], lcore.at[c], lc_s.at[0], lc_r.at[0], C, oc)

        def l_third():
            maj_wait(lmaj.at[mj], lambda i: lmaj.at[i], lj_s, lj_r)
            lcore[c] = sum([lmaj[m] for m in range(nmaj)])
            start(l_core())

        def l_out():
            remote(lcore.at[oc], lcore.at[oc], lc_s.at[0], lc_r.at[0], C, oc).wait_recv()
            total = jnp.sum(lcore[0] + lcore[1], axis=1, keepdims=True)
            loss_ref[...] = jnp.broadcast_to(total, (UNIT, LANES)) * factor

        a_first()
        x_send(xb, 0)
        l_first()
        back = x_sum(xb, 0)
        err_v[...] = ((adapter_scale_factor * coeff_v[...]) * back).astype(jnp.bfloat16)
        a_first_wait()
        a_ring_send(0)
        a_share(mj, 0)
        a_unpack(mj)
        load_act.wait()
        done = 0
        for s in range(hp):
            want = -(-blocks * (s + 1) // hp)
            while done < min(want, blocks):
                p_block(done)
                done += 1
            if s == 0:
                l_second()
            a_ring_wait(s)
            a_ring_send(s + 1)
            a_ring_use(s)
        start(p_copy())
        a_partner()
        low = jnp.zeros((tokens, LANES), jnp.float32)
        for j in range(blocks):
            part = afull[j * per_block : (j + 1) * per_block].reshape(kb, LANES).astype(jnp.bfloat16)
            low = low + jnp.dot(act[:, j * kb : (j + 1) * kb], part, preferred_element_type=jnp.float32)
        xl[x] = low.astype(jnp.bfloat16)
        x_send(xl, nx)
        l_third()
        p_copy().wait_recv()
        r_ring(0)
        r_ring(1)
        u_local()
        steps = [functools.partial(r_ring, s) for s in range(2, hp)]
        for f in steps[:1]:
            f()
        u_scatter()
        for f in steps[1:]:
            f()
        u_spread()
        r_end()
        l_out()
        u_gather()
        r_out()
        u_out()

    @pl.when(core == 0)
    def _():
        mark = len(sent)
        body(0, Z, Y)
        for copy in sent[mark:]:
            copy.wait_send()
        del sent[mark:]

    @pl.when(core == 1)
    def _():
        mark = len(sent)
        body(1, Y, Z)
        for copy in sent[mark:]:
            copy.wait_send()
        del sent[mark:]


def local(dims, activations, output_gradient, adapter_a, adapter_b, log_ratio, lengths, rewards):
    nz, ny, nx, groups, rollouts, rows, blocks, upcs = dims
    tokens, k = activations.shape
    width = output_gradient.shape[1]
    rank = adapter_b.shape[0]
    n = max(nz, ny)
    zy = nz * ny
    most = max(ny * upcs[0], nz * upcs[1])
    most_maj = max(nz * upcs[0], ny * upcs[1])
    most_other = most
    bf, f32 = jnp.bfloat16, jnp.float32
    vm, dma = pltpu.VMEM, pltpu.SemaphoreType.DMA
    ga, gb, loss = pl.pallas_call(
        functools.partial(kernel, dims),
        out_shape=(
            jax.ShapeDtypeStruct((rows, rank), f32),
            jax.ShapeDtypeStruct((rank, width), f32),
            jax.ShapeDtypeStruct((UNIT, LANES), f32),
        ),
        in_specs=[pl.BlockSpec(memory_space=pl.ANY)] * 3
        + [pl.BlockSpec(memory_space=pltpu.VMEM)] * 2
        + [pl.BlockSpec(memory_space=pltpu.SMEM)] * 2,
        out_specs=tuple([pl.BlockSpec(memory_space=pltpu.VMEM)] * 3),
        scratch_shapes=[
            vm((tokens, k), bf), vm((tokens, width), bf), vm((rank, width), bf),
            vm((tokens, rank), f32), vm((tokens, rank), f32), vm((tokens, rank), f32),
            vm((nx, tokens, rank), bf), vm((nx, tokens, rank), bf),
            vm((zy, rows, rank), bf), vm((zy, rows, rank), bf), vm((zy, 2 * rows, rank), f32),
            vm((tokens, rank), bf), vm((zy, 2 * rows, rank), f32),
            vm((zy, rows, rank), bf), vm((zy, rows, rank), bf),
            vm((zy, rows, rank), bf), vm((zy, rows, rank), bf),
            vm((n, rows, rank), f32), vm((n, rows, rank), bf), vm((n, rows, rank), bf),
            vm((rank, width), f32),
            vm((most_other, UNIT, LANES), bf), vm((most, UNIT, LANES), bf), vm((most, UNIT, LANES), bf),
            vm((most, UNIT, LANES), bf), vm((most_maj, UNIT, LANES), bf),
            vm((most, UNIT, LANES), bf), vm((most, UNIT, LANES), bf),
            vm((n, UNIT, LANES), f32), vm((n, UNIT, LANES), f32), vm((2, UNIT, LANES), f32),
            dma((3,)), dma((2 * nx,)), dma((2 * nx,)), dma((n,)), dma((n,)),
            dma((n,)), dma((n,)), dma((n,)), dma((n,)),
            dma((1,)), dma((1,)), dma((n,)), dma((n,)), dma((n,)), dma((n,)),
            dma((1,)), dma((1,)), dma((n,)), dma((n,)), dma((n,)), dma((n,)),
            dma((n,)), dma((n,)), dma((n,)), dma((n,)),
            dma((n,)), dma((n,)), dma((n,)), dma((n,)), dma((1,)), dma((1,)),
        ],
        compiler_params=pltpu.CompilerParams(
            collective_id=0, has_side_effects=True, vmem_limit_bytes=56 * 1024 * 1024
        ),
        name="grpo",
    )(
        activations, output_gradient, adapter_b, adapter_a[0],
        log_ratio.reshape(tokens // LANES, LANES), lengths, rewards,
    )
    return ga[None], gb, loss[0, 0]


def dims_of(mesh_shape, k, width, rank, groups, rollouts):
    nz, ny, nx = mesh_shape
    rows = k // (nz * ny * 2)
    zy = nz * ny
    blocks = next(
        (zy // b for b in range(16, zy + 1) if zy % b == 0 and (b * 2 * rows) % LANES == 0), 1
    )
    upcs = units_split((rank // UNIT) * (width // LANES), ny, nz)
    return (nz, ny, nx, groups, rollouts, rows, blocks, upcs)


def solution_of(mesh, nz, ny):
    nx = mesh.shape["tensor"]
    split = Mesh(mesh.devices.reshape(nz, ny, 2, nx), (Z, Y, C, X))

    def step(activations, output_gradient, adapter_a, adapter_b, log_ratio, lengths, rewards):
        dims = dims_of(
            (nz, ny, nx), activations.shape[1] // nx, output_gradient.shape[1] // nx,
            adapter_b.shape[0], *lengths.shape,
        )
        return jax.shard_map(
            functools.partial(local, dims),
            mesh=split,
            in_specs=(P(DP, X), P(DP, X), P(X, DP, None), P(None, X), P(DP), P(), P()),
            out_specs=(P(X, DP, None), P(None, X), P()),
            check_vma=False,
        )(activations, output_gradient, adapter_a, adapter_b, log_ratio, lengths, rewards)

    return step


def solution(mesh):
    return solution_of(mesh, 12, 8)
```

time: 489 us -> 97.3 us (0.20)
  waiting for transfers between devices: 346 us -> 0 us
  Pallas kernels: 0 us -> 91.8 us
  blocking collectives: 70.1 us -> 0 us
  local copies, waits for them, and re-layouts: 27.4 us -> 4.51 us
  between operations: 18.6 us -> 0.64 us
  other arithmetic: 11.5 us -> 0 us
  matrix products: 9.92 us -> 0 us
    unnamed x3 -> x0, waiting for transfers between devices: 322 us -> none
    pallas_call x0 -> x1, Pallas kernels: none -> 91.8 us  [local(): pl.pallas_call(functools.partial(kernel, dims), out_shape=(jax.ShapeDtype...]
    all_gather x4 -> x0, blocking collectives: 70.1 us -> none  [the longest x2 51.4 us: stacked_from(): blocks = lax.all_gather(blocks, axes[k])]
    all_gather x1 -> x0, waiting for transfers between devices: 18.8 us -> none  [stacked_from(): blocks = lax.all_gather(blocks, axes[k])]
    concatenate x2 -> x0, local copies, waits for them, and re-layouts: 10.2 us -> none  [the longest x1 8.46 us: packed_total(): running = lax.psum(jnp.concatenate([a.ravel() for a in arrays]), axis)]
    dot_general x4 -> x0, matrix products: 9.92 us -> none  [the longest x1 2.84 us: local(): jnp.dot(columns, gathered_by_axis(adapter_a, DP, (0, 1, 2), 1)[0], prefer...]
    all_to_all x1 -> x0, waiting for transfers between devices: 4.94 us -> none  [sent_and_summed(): lax.all_to_all(blocks, axis, split_axis=0, concat_axis=0, tiled=True)]
  transfers between devices with their start and end apart: 3 -> 0, of which waited for: 3 -> 0; matrix products, arithmetic and copies ran while one was open for 2% -> 0% of each run, Pallas kernels for 0% -> 0%
where the time goes in v1:
time: 97.3 us; the launch traced here: 97 us
  Pallas kernels  91.8 us (94%)
  local copies, waits for them, and re-layouts  4.51 us (5%)
    pallas_call x1, Pallas kernels, local(): pl.pallas_call(functools.partial(kernel, dims), out_shape=(jax.ShapeDtype...  91.8 us
    unnamed x2, local copies, waits for them, and re-layouts  3.32 us

profile of v1, /device:TPU:1, one launch (start us, length us, event | category | flops | bytes accessed | tf_op | source)
XLA Modules:
  0.0 97.0 jit_solution(2512650691788289409)
XLA Ops:
  0.6 91.8 %grpo.1 = (f32[36,128]{1,0:T(8,128)}, f32[128,1280]{1,0:T(8,128)}, f32[8,128]{1,0:T(8,128)}) custom-call(bf16[256,6912]{1,0:T(8,128)(2,1)} %act_hbm.1, bf16[256,1280]{1,0:T(8,128)(2,1)} %og_hbm.1, bf16[128,1280]{1,0:T(8,128)(2,1)} %b_hbm.1, bf16[36,128]{1,0:T(8,128)(2,1)} %bitcast.5, f32[2,128]{1,0:T(2,128)} %bitcast.6, s32[3,16]{1,0:T(4,128)} %len_ref.1, ...), custom_call_target="tpu_custom_call" | custom-call | tf_op jit(solution)/shard_map/grpo/pallas_call | solution.py:471
  92.5 1.2 %slice.3 = f32[1,1]{1,0:T(1,128)} slice(f32[8,128]{1,0:T(8,128)} %get-tuple-element.8), slice={[0:1], [0:1]} | slice | bytes 8 | tf_op jit(solution)/shard_map/slice | solution.py:511
  93.7 1.4 %copy.10 = f32[1,36,128]{2,0,1:T(1,128)} copy(f32[1,36,128]{2,1,0:T(8,128)} %bitcast.4) | data formatting | bytes 36864
  95.0 2.0 %copy.12 = f32[128,1280]{1,0:T(8,128)} copy(f32[128,1280]{1,0:T(8,128)} %get-tuple-element.16) | data formatting | bytes 1310720
